TPU v7x, 512 devices: a whole 4x8x8 slice. The times are simulated.
512 devices in a mesh: gx: 8 (over z_lo, core), gy: 8 (over y), gz: 8 (over x, z_hi).
Axes of the slice: x: 4, y: 8, z: 8 (z_hi: 2, z_lo: 4; z = z_hi * 4 + z_lo), core: 2. Of those that a mesh axis runs over, the one named last changes fastest.
Arguments:
- head_inputs: bfloat16 [131072, 2048], P(('gx', 'gy', 'gz')), may hold values from -6 to 6
- step_raw: float32 [131072, 32], P(('gx', 'gy', 'gz')), may hold values from -4 to 4
- state_in: bfloat16 [131072, 128], P(('gx', 'gy', 'gz')), may hold values from -0.119628906 to 0.119628906
- state_out: bfloat16 [131072, 128], P(('gx', 'gy', 'gz')), may hold values from -0.119628906 to 0.119628906
- decay_log: float32 [32], replicated, may hold values from -13.5 to -3
- step_bias: float32 [32], replicated, may hold values from -1 to 0.5
- skip_gain: float32 [32], replicated, may hold values from 0.5 to 1.5
- checkpoints: bfloat16 [512, 32, 64, 128], P(('gx', 'gy'), None, 'gz'), may hold values from -6 to 6
- out_grad: bfloat16 [131072, 2048], P(('gx', 'gy', 'gz')), may hold values from -6 to 6
Outputs:
- input_grad: bfloat16 [131072, 2048], P(('gx', 'gy', 'gz'))
- step_grad: float32 [131072, 32], P(('gx', 'gy', 'gz'))
- state_in_grad: float32 [131072, 128], P(('gx', 'gy', 'gz'))
- state_out_grad: float32 [131072, 128], P(('gx', 'gy', 'gz'))
- decay_log_grad: float32 [32], replicated
- step_bias_grad: float32 [32], replicated
- skip_gain_grad: float32 [32], replicated
All inputs are finite; a program needn't handle non-finite values.
Results may differ from a plain program's by a relative error of at most 0.00065.
Values may be sent and summed in bfloat16 or wider, within the bound.
A program may use at most 128 MiB of HBM per device.

v0:
```python
import jax
import jax.numpy as jnp
from jax import lax
from jax.sharding import Mesh
from jax.sharding import PartitionSpec as P

GZ = ("gz_0", "gz_1")
GX_GY = ("gx_0", "gx_1", "gy")
GX_GY_GZ = ("gx_0", "gx_1", "gy", "gz_0", "gz_1")
highest = lax.Precision.HIGHEST


def neutral_like(array, identity):
    return jax.tree.map(
        lambda a, e: jnp.broadcast_to(jnp.asarray(e, a.dtype), a.shape), array, identity
    )


def carried_in(array, axes, combine, identity):
    before = start = neutral_like(array, identity)
    so_far = array
    for axis in reversed(axes):
        length, index = (lax.axis_size(axis), lax.axis_index(axis))
        pieces = jax.tree.map(lambda part: lax.all_gather(part, axis), so_far)
        inside, so_far = (start, start)
        for k in reversed(range(length)):
            passed = k > index
            so_far = combine(so_far, jax.tree.map(lambda part: part[k], pieces))
            inside = jax.tree.map(lambda new, old: jnp.where(passed, new, old), so_far, inside)
        before = combine(inside, before)
    return before


def by_axis(array, axes):
    for axis in axes:
        array = lax.psum(array, axis)
    return array


def block_forward(inputs, raw, b_mat, scores, read, decay_log, bias, skip, start):
    step = jax.nn.softplus(raw + bias)
    cum = jnp.cumsum(step * -jnp.exp(decay_log), axis=0)
    length = inputs.shape[0]
    rows = lax.broadcasted_iota(jnp.int32, (length, length), 0)
    cols = lax.broadcasted_iota(jnp.int32, (length, length), 1)
    lower = rows >= cols
    ctrans = cum.T
    gap = ctrans[:, :, None] - ctrans[:, None, :]
    mix = jnp.where(lower, jnp.exp(jnp.where(lower, gap, 0.0)), 0.0) * scores * step.T[:, None, :]
    inner = jnp.einsum("hts,shp->thp", mix, inputs, precision=highest)
    carried = read * jnp.exp(cum)[:, :, None]
    result = inner + carried + skip[None, :, None] * inputs
    tail = jnp.exp(cum[-1][None, :] - cum) * step
    final = jnp.exp(cum[-1])[:, None, None] * start + jnp.einsum(
        "sh,shp,sn->hpn", tail, inputs, b_mat, precision=highest
    )
    return (result, final)


def span_forward(inputs, raw, b_mat, scores, read, decay_log, bias, skip, start):
    length, heads = raw.shape
    width = inputs.shape[1] // heads
    states = start.shape[2]
    block = min(8, heads)
    blocks = heads // block
    grouped = inputs.reshape(length, blocks, block, width).transpose(1, 0, 2, 3)
    read_g = read.reshape(length, blocks, block, width).transpose(1, 0, 2, 3)
    raw_g = raw.reshape(length, blocks, block).transpose(1, 0, 2)

    def one_block(items):
        return block_forward(
            items[0], items[1], b_mat, scores, items[2], items[3], items[4], items[5], items[6]
        )

    result, final = lax.map(
        one_block,
        (
            grouped,
            raw_g,
            read_g,
            decay_log.reshape(blocks, block),
            bias.reshape(blocks, block),
            skip.reshape(blocks, block),
            start.reshape(blocks, block, width, states),
        ),
    )
    result = result.transpose(1, 0, 2, 3).reshape(length, heads * width)
    return (result, final.reshape(heads, width, states))


def combine(earlier, later):
    return (earlier[0] * later[0], later[0][:, None, None] * earlier[1] + later[1])


def local(
    head_inputs,
    step_raw,
    state_in,
    state_out,
    decay_log,
    step_bias,
    skip_gain,
    checkpoints,
    out_grad,
):
    entering = lax.all_to_all(checkpoints, GZ, split_axis=0, concat_axis=2, tiled=True)[0]
    start = entering.astype(jnp.float32)
    length, heads = step_raw.shape
    width = head_inputs.shape[1] // heads
    states = state_in.shape[1]
    c_mat = state_out.astype(jnp.float32)
    b_mat = state_in.astype(jnp.float32)
    grad_rows = out_grad.astype(jnp.float32)
    step = jax.nn.softplus(step_raw + step_bias)
    cum = jnp.cumsum(step * -jnp.exp(decay_log), axis=0)
    weighted = (grad_rows.reshape(length, heads, width) * jnp.exp(cum)[:, :, None]).reshape(
        length, heads * width
    )
    local_term = jnp.dot(weighted.T, c_mat, precision=highest).reshape(heads, width, states)
    decays = jnp.exp(cum[-1])
    group = lax.axis_size(GZ)
    spread = jnp.broadcast_to(decays[None, :, None], (1, heads, group))
    got_decay, got_term = (
        lax.all_to_all(spread, GZ, split_axis=2, concat_axis=0, tiled=True),
        lax.all_to_all(local_term[None], GZ, split_axis=2, concat_axis=0, tiled=True),
    )
    got_decay = got_decay[:, :, 0]
    slice_width = got_term.shape[2]
    suffix_b = jnp.zeros((heads, slice_width, states), jnp.float32)
    suffix_a = jnp.ones((heads,), jnp.float32)
    inners = [None] * group
    leads = [None] * group
    for member in reversed(range(group)):
        inners[member] = suffix_b
        leads[member] = suffix_a
        suffix_b = got_term[member] + got_decay[member][:, None, None] * suffix_b
        suffix_a = got_decay[member] * suffix_a
    total = (suffix_a, suffix_b)
    neutral = (
        jnp.ones((heads,), jnp.float32),
        jnp.zeros((heads, slice_width, states), jnp.float32),
    )
    outer = carried_in(total, GX_GY, combine, neutral)
    carries = jnp.stack(
        [inners[member] + leads[member][:, None, None] * outer[1] for member in range(group)]
    )
    later = lax.all_to_all(carries, GZ, split_axis=0, concat_axis=2, tiled=True)[0]
    flat_start = entering.reshape(heads * width, states)
    scores = jnp.dot(state_out, state_in.T, preferred_element_type=jnp.float32)
    read = jnp.dot(state_out, flat_start.T, preferred_element_type=jnp.float32)
    _, pull = jax.vjp(
        span_forward,
        head_inputs.astype(jnp.float32),
        step_raw,
        b_mat,
        scores,
        read,
        decay_log,
        step_bias,
        skip_gain,
        start,
    )
    grads = pull((grad_rows, later))
    b_grad = grads[2] + jnp.dot(grads[3].T, c_mat, precision=highest)
    c_grad = jnp.dot(grads[3], b_mat, precision=highest) + jnp.dot(
        grads[4], flat_start.astype(jnp.float32), precision=highest
    )
    decay_sum, bias_sum, skip_sum = (
        by_axis(grads[5], GX_GY_GZ),
        by_axis(grads[6], GX_GY_GZ),
        by_axis(grads[7], GX_GY_GZ),
    )
    return (grads[0].astype(jnp.bfloat16), grads[1], b_grad, c_grad, decay_sum, bias_sum, skip_sum)


def solution(mesh):
    torus = Mesh(
        mesh.devices.reshape(4, 2, mesh.shape["gy"], 4, 2), ("gx_0", "gx_1", "gy", "gz_0", "gz_1")
    )
    return jax.shard_map(
        local,
        mesh=torus,
        in_specs=(
            P(GX_GY_GZ, None),
            P(GX_GY_GZ, None),
            P(GX_GY_GZ, None),
            P(GX_GY_GZ, None),
            P(),
            P(),
            P(),
            P(GX_GY, None, GZ, None),
            P(GX_GY_GZ, None),
        ),
        out_specs=(
            P(GX_GY_GZ, None),
            P(GX_GY_GZ, None),
            P(GX_GY_GZ, None),
            P(GX_GY_GZ, None),
            P(),
            P(),
            P(),
        ),
        check_vma=False,
    )
```

profile of v0, /device:TPU:64, one launch (start us, length us, event | category | flops | bytes accessed | tf_op | source)
XLA Modules:
  0.0 441.4 jit_solution(9832343445623595339)
XLA Ops:
  10.4 11.8 %all-to-all-start.1 = ((f32[1,32,8]{1,0,2:T(1,128)}), f32[1,32,8]{1,0,2:T(1,128)S(1)}, u32[]{:S(2)}, u32[]{:S(2)}) async-start(f32[1,32,8]{1,0,2:T(1,128)} %broadcast_in_dim.210), calls=%async_computation.1 | async-start | bytes 8192 | tf_op jit(solution)/shard_map/all_to_all | solution.py:124
  22.4 1.5 copy.168
  25.1 1.6 copy.171
  26.7 5.6 %all-to-all-done.1 = f32[1,32,8]{1,0,2:T(1,128)S(1)} async-done(((f32[1,32,8]{1,0,2:T(1,128)}), f32[1,32,8]{1,0,2:T(1,128)S(1)}, u32[]{:S(2)}, u32[]{:S(2)}) %all-to-all-start.1) | async-done | bytes 1056 | tf_op jit(solution)/shard_map/all_to_all | solution.py:124
  32.3 4.0 all-to-all-start
  37.5 29.1 %all-to-all-done = f32[1,32,64,128]{3,1,0,2:T(8,128)S(1)} async-done(((f32[1,32,64,128]{3,1,0,2:T(8,128)}), f32[1,32,64,128]{3,1,0,2:T(8,128)S(1)}, u32[]{:S(2)}, u32[]{:S(2)}) %all-to-all-start) | async-done | bytes 1048608 | tf_op jit(solution)/shard_map/all_to_all | solution.py:125
  68.3 4.2 all-to-all-start.3
  73.4 2.6 copy.164
  76.8 16.8 %all-gather = f32[8,1,32,1]{2,3,1,0:T(1,128)S(1)} all-gather(f32[1,1,32,1]{2,3,1,0:T(1,128)S(1)} %get-tuple-element.1868), channel_id=2, replica_groups=mesh['gx_0'=4,'gx_1'=2,'gy'=8,'gz_0'=4,'gz_1'=2] {'gy'}, dimensions={0}, use_global_device_ids=true | all-gather | bytes 1152 | tf_op jit(solution)/shard_map/all_gather | solution.py:24
  93.6 1.8 all-gather.1
  95.4 8.2 %all-gather.2 = f32[4,1,32]{2,1,0:T(1,128)S(1)} all-gather(f32[1,1,32]{2,1,0:T(1,128)S(1)} %get-tuple-element.1888), channel_id=1, replica_groups=mesh['gx_0'=4,'gx_1'=2,'gy'=8,'gz_0'=4,'gz_1'=2] {'gx_0'}, dimensions={0}, use_global_device_ids=true | all-gather | bytes 640 | tf_op jit(solution)/shard_map/all_gather | solution.py:24
  105.9 1.7 slice_add_fusion.6
  107.7 2.1 all_gather.28
  110.0 16.5 %all_gather.29 = f32[4,32,8,128]{3,2,1,0:T(8,128)S(1)} all-gather(f32[1,32,8,128]{3,2,1,0:T(8,128)S(1)} %slice_add_fusion.4), channel_id=1, replica_groups=mesh['gx_0'=4,'gx_1'=2,'gy'=8,'gz_0'=4,'gz_1'=2] {'gx_0'}, dimensions={0}, use_global_device_ids=true | all-gather | bytes 655360 | tf_op jit(solution)/shard_map/all_gather | solution.py:24
  126.6 2.2 add_dynamic-update-slice_fusion.6
  134.1 6.5 %all-to-all-start.2 = ((f32[8,32,8,128]{3,2,1,0:T(8,128)}), f32[8,32,8,128]{3,2,1,0:T(8,128)}, u32[]{:S(2)}, u32[]{:S(2)}) async-start(f32[8,32,8,128]{3,2,1,0:T(8,128)} %constant_dynamic-update-slice_fusion.3), calls=%async_computation.2 | async-start | bytes 2097152 | tf_op jit(solution)/shard_map/all_to_all | solution.py:147
  140.6 1.5 broadcast.740.clone.1
  145.8 57.4 %while.75 = (s32[]{:T(128)}, f32[4,256,8]{1,2,0:T(8,128)}, f32[4,8]{1,0:T(4,128)}, f32[4,1,8]{2,1,0:T(1,128)}, f32[4,256,8]{1,2,0:T(8,128)}, /*index=5*/f32[4,8,...) while((s32[]{:T(128)}, f32[4,256,8]{1,2,0:T(8,128)}, ...), condition=%wide.region_5.6_spmd.clone.clone, body=%wide.region_2.5_spmd.clone.clone.sunk | while | flops 3090474 | bytes 14180141 | solution.py:75
  147.4 4.2 multiply_dynamic-update-slice_fusion.4
  161.8 4.0 multiply_dynamic-update-slice_fusion.4
  176.1 4.2 multiply_dynamic-update-slice_fusion.4
  190.5 4.0 multiply_dynamic-update-slice_fusion.4
  208.8 1.8 convolution_bitcast_fusion.2
  210.5 2.3 copy.181
  212.9 1.6 broadcast.740
  216.8 157.2 %while.76 = (s32[]{:T(128)}, f32[256,256]{1,0:T(8,128)S(1)}, f32[256,128]{1,0:T(8,128)}, bf16[4,256,8,64]{1,3,2,0:T(8,128)(2,1)}, f32[4,256,8]{1,2,0:T(8,128)}, ...) while((s32[]{:T(128)}, f32[256,256]{1,0:T(8,128)S(1)}, ...), condition=%wide.region_19.20_spmd.clone.clone, body=%wide.region_6.19_spmd.clone.clone.sunk | while | flops 1215725568 | bytes 18326480 | solution.py:75
  217.4 2.5 fusion.152
  222.0 6.5 %fusion.150 = (f32[8,256]{1,0:T(8,128)}, f32[8,256]{1,0:T(8,128)}, f32[256,256]{1,0:T(8,128)S(1)}, f32[8,256]{1,0:T(8,128)}) fusion(f32[4,8,256,256]{3,2,1,0:T(8,128)} %get-tuple-element.2474, s32[]{:T(128)S(6)} %sub.146, f32[256,256]{1,0:T(8,128)S(1)} %bitcast.579, f32[8,256]{1,0:T(8,128)S(1)} %dynamic-slice_bitcast_fusion.6, ...), kind=kOutput, calls=%fused_computation.87.clone.1 | convolution fusion | flops 408348672 | bytes 7964160 | tf_op jit(solution)/shard_map/transpose(jvp())/while/body/eval_jaxpr/hts,shp->thp/dot_general | solution.py:50
  228.5 1.7 fusion.157
  232.3 1.4 fusion.159
  233.7 3.2 reduce-window.62
  240.1 1.4 fusion.160
  246.7 3.7 fusion.154
  253.3 2.8 fusion.151
  256.6 2.5 fusion.152
  261.3 6.5 %fusion.150 = (f32[8,256]{1,0:T(8,128)}, f32[8,256]{1,0:T(8,128)}, f32[256,256]{1,0:T(8,128)S(1)}, f32[8,256]{1,0:T(8,128)}) fusion(f32[4,8,256,256]{3,2,1,0:T(8,128)} %get-tuple-element.2474, s32[]{:T(128)S(6)} %sub.146, f32[256,256]{1,0:T(8,128)S(1)} %bitcast.579, f32[8,256]{1,0:T(8,128)S(1)} %dynamic-slice_bitcast_fusion.6, ...), kind=kOutput, calls=%fused_computation.87.clone.1 | convolution fusion | flops 408348672 | bytes 7964160 | tf_op jit(solution)/shard_map/transpose(jvp())/while/body/eval_jaxpr/hts,shp->thp/dot_general | solution.py:50
  267.8 1.7 fusion.157
  273.0 3.2 reduce-window.62
  279.3 1.4 fusion.160
  286.0 3.7 fusion.154
  292.5 2.8 fusion.151
  295.9 2.5 fusion.152
  300.6 6.5 %fusion.150 = (f32[8,256]{1,0:T(8,128)}, f32[8,256]{1,0:T(8,128)}, f32[256,256]{1,0:T(8,128)S(1)}, f32[8,256]{1,0:T(8,128)}) fusion(f32[4,8,256,256]{3,2,1,0:T(8,128)} %get-tuple-element.2474, s32[]{:T(128)S(6)} %sub.146, f32[256,256]{1,0:T(8,128)S(1)} %bitcast.579, f32[8,256]{1,0:T(8,128)S(1)} %dynamic-slice_bitcast_fusion.6, ...), kind=kOutput, calls=%fused_computation.87.clone.1 | convolution fusion | flops 408348672 | bytes 7964160 | tf_op jit(solution)/shard_map/transpose(jvp())/while/body/eval_jaxpr/hts,shp->thp/dot_general | solution.py:50
  307.1 1.7 fusion.157
  312.3 3.2 reduce-window.62
  318.6 1.4 fusion.160
  325.3 3.7 fusion.154
  331.9 2.8 fusion.151
  335.2 2.5 fusion.152
  339.9 6.5 %fusion.150 = (f32[8,256]{1,0:T(8,128)}, f32[8,256]{1,0:T(8,128)}, f32[256,256]{1,0:T(8,128)S(1)}, f32[8,256]{1,0:T(8,128)}) fusion(f32[4,8,256,256]{3,2,1,0:T(8,128)} %get-tuple-element.2474, s32[]{:T(128)S(6)} %sub.146, f32[256,256]{1,0:T(8,128)S(1)} %bitcast.579, f32[8,256]{1,0:T(8,128)S(1)} %dynamic-slice_bitcast_fusion.6, ...), kind=kOutput, calls=%fused_computation.87.clone.1 | convolution fusion | flops 408348672 | bytes 7964160 | tf_op jit(solution)/shard_map/transpose(jvp())/while/body/eval_jaxpr/hts,shp->thp/dot_general | solution.py:50
  346.4 1.7 fusion.157
  350.1 1.4 fusion.159
  351.6 3.2 reduce-window.62
  358.0 1.4 fusion.160
  364.6 3.7 fusion.154
  371.2 2.8 fusion.151
  377.5 1.9 convolution_add_fusion.1
  379.5 2.3 copy.184
  381.7 11.6 %all-reduce.4 = (f32[32]{0:T(128)S(1)}, f32[32]{0:T(128)S(1)}, f32[32]{0:T(128)S(1)}) all-reduce(f32[32]{0:T(128)S(1)} %reshape.895, f32[32]{0:T(128)S(1)} %reshape.896, f32[32]{0:T(128)S(1)} %reshape.897), channel_id=1, replica_groups=mesh['gx_0'=4,'gx_1'=2,'gy'=8,'gz_0'=4,'gz_1'=2] {'gx_0'}, use_global_device_ids=true, to_apply=%region_20.21 | all-reduce | flops 96 | bytes 768 | tf_op jit(solution)/shard_map/psum | solution.py:36
  393.3 2.5 all-reduce.6
  395.8 16.1 %all-reduce.2 = (f32[32]{0:T(128)S(1)}, f32[32]{0:T(128)S(1)}, f32[32]{0:T(128)S(1)}) all-reduce(f32[32]{0:T(128)S(1)} %get-tuple-element.1825, f32[32]{0:T(128)S(1)} %get-tuple-element.1826, f32[32]{0:T(128)S(1)} %get-tuple-element.1827), channel_id=1, replica_groups=mesh['gx_0'=4,'gx_1'=2,'gy'=8,'gz_0'=4,'gz_1'=2] {'gy'}, use_global_device_ids=true, to_apply=%region_22.23 | all-reduce | flops 96 | bytes 768 | tf_op jit(solution)/shard_map/psum | solution.py:36
  411.8 10.9 %all-reduce.3 = (f32[32]{0:T(128)S(1)}, f32[32]{0:T(128)S(1)}, f32[32]{0:T(128)S(1)}) all-reduce(f32[32]{0:T(128)S(1)} %get-tuple-element.1813, f32[32]{0:T(128)S(1)} %get-tuple-element.1814, f32[32]{0:T(128)S(1)} %get-tuple-element.1815), channel_id=1, replica_groups=mesh['gx_0'=4,'gx_1'=2,'gy'=8,'gz_0'=4,'gz_1'=2] {'gz_0'}, use_global_device_ids=true, to_apply=%region_23.24 | all-reduce | flops 96 | bytes 768 | tf_op jit(solution)/shard_map/psum | solution.py:36
  422.8 9.3 %all-reduce.5 = (f32[32]{0:T(128)}, f32[32]{0:T(128)}, f32[32]{0:T(128)}) all-reduce(f32[32]{0:T(128)S(1)} %get-tuple-element.1816, f32[32]{0:T(128)S(1)} %get-tuple-element.1817, f32[32]{0:T(128)S(1)} %get-tuple-element.1818), channel_id=1, replica_groups=mesh['gx_0'=4,'gx_1'=2,'gy'=8,'gz_0'=4,'gz_1'=2] {'gz_1'}, use_global_device_ids=true, to_apply=%region_24.25 | all-reduce | flops 96 | bytes 768 | tf_op jit(solution)/shard_map/psum | solution.py:36
  432.1 2.5 convolution_add_fusion
  (340 shorter events, 139.8 us)
Async XLA Ops:
  7.2 16.8 %copy-start = (bf16[256,128]{1,0:T(8,128)(2,1)S(1)}, bf16[256,128]{1,0:T(8,128)(2,1)}, u32[]{:S(2)}) copy-start(bf16[256,128]{1,0:T(8,128)(2,1)} %param.16) | copy-start | bytes 196612
  10.4 21.9 %all-to-all-start.1 = ((f32[1,32,8]{1,0,2:T(1,128)}), f32[1,32,8]{1,0,2:T(1,128)S(1)}, u32[]{:S(2)}, u32[]{:S(2)}) async-start(f32[1,32,8]{1,0,2:T(1,128)} %broadcast_in_dim.210), calls=%async_computation.1 | async-start | bytes 8192 | tf_op jit(solution)/shard_map/all_to_all | solution.py:124
  23.8 1.2 copy-start.1
  32.3 34.3 %all-to-all-start = ((f32[1,32,64,128]{3,1,0,2:T(8,128)}), f32[1,32,64,128]{3,1,0,2:T(8,128)S(1)}, u32[]{:S(2)}, u32[]{:S(2)}) async-start(f32[1,32,64,128]{3,1,0,2:T(8,128)} %copy.171), calls=%async_computation | async-start | bytes 2097152 | tf_op jit(solution)/shard_map/all_to_all | solution.py:125
  36.3 69.5 %all-gather.5.cloned.1.call-start = ((), (), s32[]{:S(2)}) async-start(), calls=%async_computation.4 | async-start | bytes 1179648 | tf_op jit(solution)/shard_map/all_gather | solution.py:24
  37.0 31.3 %copy-start.18 = (f32[32]{0:T(128)}, f32[32]{0:T(128)S(1)}, u32[]{:S(2)}) copy-start(f32[32]{0:T(128)S(1)} %get-tuple-element.1883) | copy-start | bytes 388
  37.4 30.9 %copy-start.20 = (f32[32]{0:T(128)}, f32[32]{0:T(128)S(1)}, u32[]{:S(2)}) copy-start(f32[32]{0:T(128)S(1)} %get-tuple-element.1874) | copy-start | bytes 388
  37.4 30.9 %copy-start.22 = (f32[32]{0:T(128)}, f32[32]{0:T(128)S(1)}, u32[]{:S(2)}) copy-start(f32[32]{0:T(128)S(1)} %get-tuple-element.1870) | copy-start | bytes 388
  37.4 30.9 %copy-start.24 = (f32[32]{0:T(128)}, f32[32]{0:T(128)S(1)}, u32[]{:S(2)}) copy-start(f32[32]{0:T(128)S(1)} %get-tuple-element.1872) | copy-start | bytes 388
  37.4 35.2 %copy-start.31 = (f32[32]{0:T(128)S(1)}, f32[32]{0:T(128)}, u32[]{:S(2)}) copy-start(f32[32]{0:T(128)} %param.18) | copy-start | bytes 388
  37.5 35.8 %copy-start.41 = (f32[32]{0:T(128)S(1)}, f32[32]{0:T(128)}, u32[]{:S(2)}) copy-start(f32[32]{0:T(128)} %param.17) | copy-start | bytes 388
  68.3 7.7 %copy-start.42 = (f32[32]{0:T(128)S(1)}, f32[32]{0:T(128)}, u32[]{:S(2)}) copy-start(f32[32]{0:T(128)} %param.19) | copy-start | bytes 388
  68.3 8.3 %copy-start.9 = (bf16[256,128]{1,0:T(8,128)(2,1)S(1)}, bf16[256,128]{1,0:T(8,128)(2,1)}, u32[]{:S(2)}) copy-start(bf16[256,128]{1,0:T(8,128)(2,1)} %param.15) | copy-start | bytes 196612
  68.3 65.7 %all-to-all-start.3 = ((bf16[8,32,8,128]{3,2,1,0:T(8,128)(2,1)}), bf16[8,32,8,128]{3,2,1,0:T(8,128)(2,1)}, u32[]{:S(2)}, u32[]{:S(2)}) async-start(bf16[8,32,8,128]{3,2,1,0:T(8,128)(2,1)} %param.20), calls=%async_computation.3 | async-start | bytes 1048576 | tf_op jit(solution)/shard_map/all_to_all | solution.py:106
  93.6 14.0 %copy-start.14 = (f32[32]{0:T(128)}, f32[32]{0:T(128)S(1)}, u32[]{:S(2)}) copy-start(f32[32]{0:T(128)S(1)} %get-tuple-element.1878) | copy-start | bytes 388
  93.6 14.0 %copy-start.15 = (f32[32]{0:T(128)}, f32[32]{0:T(128)S(1)}, u32[]{:S(2)}) copy-start(f32[32]{0:T(128)S(1)} %get-tuple-element.1879) | copy-start | bytes 388
  93.6 14.0 %copy-start.16 = (f32[32]{0:T(128)}, f32[32]{0:T(128)S(1)}, u32[]{:S(2)}) copy-start(f32[32]{0:T(128)S(1)} %get-tuple-element.1881) | copy-start | bytes 388
  93.6 14.0 %copy-start.17 = (f32[32]{0:T(128)}, f32[32]{0:T(128)S(1)}, u32[]{:S(2)}) copy-start(f32[32]{0:T(128)S(1)} %get-tuple-element.1882) | copy-start | bytes 388
  95.4 14.4 %copy-start.21 = (f32[32]{0:T(128)}, f32[32]{0:T(128)S(1)}, u32[]{:S(2)}) copy-start(f32[32]{0:T(128)S(1)} %get-tuple-element.1889) | copy-start | bytes 388
  103.6 4.0 copy-start.26
  103.6 6.2 %copy-start.27 = (f32[32]{0:T(128)}, f32[32]{0:T(128)S(1)}, u32[]{:S(2)}) copy-start(f32[32]{0:T(128)S(1)} %bitcast_multiply_fusion.17) | copy-start | bytes 388
  105.8 20.7 %copy-start.5 = (f32[8,32,8,128]{3,2,1,0:T(8,128)S(1)}, f32[8,32,8,128]{3,2,1,0:T(8,128)}, u32[]{:S(2)}) copy-start(f32[8,32,8,128]{3,2,1,0:T(8,128)} %all-gather.5.cloned.1.call-done) | copy-start | bytes 3145732
  105.8 20.7 %copy-start.33 = (f32[32]{0:T(128)S(1)}, f32[32]{0:T(128)}, u32[]{:S(2)}) copy-start(f32[32]{0:T(128)} %get-tuple-element.1844) | copy-start | bytes 388
  105.8 20.7 %copy-start.34 = (f32[32]{0:T(128)S(1)}, f32[32]{0:T(128)}, u32[]{:S(2)}) copy-start(f32[32]{0:T(128)} %get-tuple-element.1845) | copy-start | bytes 388
  105.8 20.7 %copy-start.35 = (f32[32]{0:T(128)S(1)}, f32[32]{0:T(128)}, u32[]{:S(2)}) copy-start(f32[32]{0:T(128)} %get-tuple-element.1884) | copy-start | bytes 388
  105.8 20.7 %copy-start.36 = (f32[32]{0:T(128)S(1)}, f32[32]{0:T(128)}, u32[]{:S(2)}) copy-start(f32[32]{0:T(128)} %get-tuple-element.1885) | copy-start | bytes 388
  105.8 20.7 %copy-start.37 = (f32[32]{0:T(128)S(1)}, f32[32]{0:T(128)}, u32[]{:S(2)}) copy-start(f32[32]{0:T(128)} %get-tuple-element.1886) | copy-start | bytes 388
  105.9 20.7 %copy-start.38 = (f32[32]{0:T(128)S(1)}, f32[32]{0:T(128)}, u32[]{:S(2)}) copy-start(f32[32]{0:T(128)} %get-tuple-element.1887) | copy-start | bytes 388
  107.6 21.2 %copy-start.30 = (f32[32]{0:T(128)S(1)}, f32[32]{0:T(128)}, u32[]{:S(2)}) copy-start(f32[32]{0:T(128)} %get-tuple-element.1839) | copy-start | bytes 388
  107.6 21.9 %copy-start.7 = (f32[1,32,8,128]{3,2,1,0:T(8,128)S(1)}, f32[1,32,8,128]{3,2,1,0:T(8,128)}, u32[]{:S(2)}) copy-start(f32[1,32,8,128]{3,2,1,0:T(8,128)} %get-tuple-element.1850) | copy-start | bytes 393220
  107.6 21.9 %copy-start.25 = (f32[32]{0:T(128)S(1)}, f32[32]{0:T(128)}, u32[]{:S(2)}) copy-start(f32[32]{0:T(128)} %copy-done.24) | copy-start | bytes 388
  107.7 21.9 %copy-start.40 = (f32[32]{0:T(128)S(1)}, f32[32]{0:T(128)}, u32[]{:S(2)}) copy-start(f32[32]{0:T(128)} %get-tuple-element.1840) | copy-start | bytes 388
  109.8 20.5 %copy-start.29 = (f32[32]{0:T(128)S(1)}, f32[32]{0:T(128)}, u32[]{:S(2)}) copy-start(f32[32]{0:T(128)} %get-tuple-element.1841) | copy-start | bytes 388
  109.9 21.2 %copy-start.6 = (f32[1,32,8,128]{3,2,1,0:T(8,128)S(1)}, f32[1,32,8,128]{3,2,1,0:T(8,128)}, u32[]{:S(2)}) copy-start(f32[1,32,8,128]{3,2,1,0:T(8,128)} %get-tuple-element.1851) | copy-start | bytes 393220
  109.9 21.1 %copy-start.23 = (f32[32]{0:T(128)S(1)}, f32[32]{0:T(128)}, u32[]{:S(2)}) copy-start(f32[32]{0:T(128)} %copy-done.22) | copy-start | bytes 388
  110.0 21.1 %copy-start.39 = (f32[32]{0:T(128)S(1)}, f32[32]{0:T(128)}, u32[]{:S(2)}) copy-start(f32[32]{0:T(128)} %get-tuple-element.1842) | copy-start | bytes 388
  126.5 5.3 %copy-start.28 = (f32[32]{0:T(128)S(1)}, f32[32]{0:T(128)}, u32[]{:S(2)}) copy-start(f32[32]{0:T(128)} %get-tuple-element.1843) | copy-start | bytes 388
  126.5 6.1 %copy-start.19 = (f32[32]{0:T(128)S(1)}, f32[32]{0:T(128)}, u32[]{:S(2)}) copy-start(f32[32]{0:T(128)} %copy-done.18) | copy-start | bytes 388
  126.6 6.1 %copy-start.32 = (f32[32]{0:T(128)S(1)}, f32[32]{0:T(128)}, u32[]{:S(2)}) copy-start(f32[32]{0:T(128)} %get-tuple-element.1866) | copy-start | bytes 388
  134.0 11.7 %copy-start.8 = (f32[256,32]{0,1:T(8,128)S(1)}, f32[256,32]{0,1:T(8,128)}, u32[]{:S(2)}) copy-start(f32[256,32]{0,1:T(8,128)} %param.14) | copy-start | bytes 98308
  134.1 76.5 %all-to-all-start.2 = ((f32[8,32,8,128]{3,2,1,0:T(8,128)}), f32[8,32,8,128]{3,2,1,0:T(8,128)}, u32[]{:S(2)}, u32[]{:S(2)}) async-start(f32[8,32,8,128]{3,2,1,0:T(8,128)} %constant_dynamic-update-slice_fusion.3), calls=%async_computation.2 | async-start | bytes 2097152 | tf_op jit(solution)/shard_map/all_to_all | solution.py:147
  203.1 1.4 copy-start.10
  207.6 3.0 copy-start.3
  216.8 0.6 copy-start.11
  246.7 3.8 copy-start.13
  250.4 5.6 %copy-start.12 = (f32[4,8]{0,1:T(8,128)S(1)}, f32[4,8]{0,1:T(8,128)}, u32[]{:S(2)}) copy-start(f32[4,8]{0,1:T(8,128)} %copy-done.11) | copy-start | bytes 388 | tf_op jit(solution)/shard_map/transpose(jvp())/while
  256.1 0.6 copy-start.11
  286.0 3.8 copy-start.13
  289.7 5.7 %copy-start.12 = (f32[4,8]{0,1:T(8,128)S(1)}, f32[4,8]{0,1:T(8,128)}, u32[]{:S(2)}) copy-start(f32[4,8]{0,1:T(8,128)} %copy-done.11) | copy-start | bytes 388 | tf_op jit(solution)/shard_map/transpose(jvp())/while
  295.3 0.6 copy-start.11
  325.3 3.8 copy-start.13
  329.0 5.7 %copy-start.12 = (f32[4,8]{0,1:T(8,128)S(1)}, f32[4,8]{0,1:T(8,128)}, u32[]{:S(2)}) copy-start(f32[4,8]{0,1:T(8,128)} %copy-done.11) | copy-start | bytes 388 | tf_op jit(solution)/shard_map/transpose(jvp())/while
  334.7 0.6 copy-start.11
  364.6 3.8 copy-start.13
  368.3 5.7 %copy-start.12 = (f32[4,8]{0,1:T(8,128)S(1)}, f32[4,8]{0,1:T(8,128)}, u32[]{:S(2)}) copy-start(f32[4,8]{0,1:T(8,128)} %copy-done.11) | copy-start | bytes 388 | tf_op jit(solution)/shard_map/transpose(jvp())/while
  374.0 58.1 %copy-start.2 = (f32[4,256,8,64]{1,3,2,0:T(8,128)S(1)}, f32[4,256,8,64]{1,3,2,0:T(8,128)}, u32[]{:S(2)}) copy-start(f32[4,256,8,64]{1,3,2,0:T(8,128)} %get-tuple-element.1033) | copy-start | bytes 6291460
  374.0 58.1 %copy-start.4 = (bf16[8,32,8,128]{3,2,0,1:T(8,128)(2,1)S(1)}, bf16[8,32,8,128]{3,2,0,1:T(8,128)(2,1)}, u32[]{:S(2)}) copy-start(bf16[8,32,8,128]{3,2,0,1:T(8,128)(2,1)} %copy-done.3) | copy-start | bytes 1572868
Sparse Core Ops, SparseCore 0:
  68.4 37.3 all-gather.4
where the time goes:
time: 445 us; the launch traced here: 441 us
  local copies, waits for them, and re-layouts  99.1 us (22%)
  other arithmetic  98.9 us (22%)
  blocking collectives  95.8 us (22%)
  matrix products  70.4 us (16%)
  waiting for transfers between devices  35.7 us (8%)
  starting transfers between devices  26.6 us (6%)
  between operations  14.6 us (3%)
    psum x5, blocking collectives, by_axis(): array = lax.psum(array, axis)  50.4 us
    all_gather x5, blocking collectives, carried_in(): pieces = jax.tree.map(lambda part: lax.all_gather(part, axis), so_far)  45.4 us
    dot_general x8, matrix products, block_forward(): inner = jnp.einsum('hts,shp->thp', mix, inputs, precision=highest)  40.7 us
    dynamic_update_slice x36, local copies, waits for them, and re-layouts, span_forward(): lax.map(one_block, (grouped, raw_g, read_g, decay_log.reshape(blocks, blo...  32.7 us
    dynamic_update_slice x24, other arithmetic, span_forward(): lax.map(one_block, (grouped, raw_g, read_g, decay_log.reshape(blocks, blo...  30.3 us
    all_to_all x1, waiting for transfers between devices, local(): lax.all_to_all(local_term[None], GZ, split_axis=2, concat_axis=0, tiled=T...  29.1 us
    another operation x33, other arithmetic  27.8 us
    dot_general x8, matrix products, block_forward(): jnp.einsum('sh,shp,sn->hpn', tail, inputs, b_mat, precision=highest)  21.1 us
  transfers between devices with their start and end apart: 5, of which 3 were waited for; matrix products, arithmetic and copies ran while one was open for 20% of the time, Pallas kernels for 0%

commit v1 on v0

--- a/solution.py
+++ b/solution.py
@@ -122,7 +122,15 @@
     spread = jnp.broadcast_to(decays[None, :, None], (1, heads, group))
     got_decay, got_term = (
         lax.all_to_all(spread, GZ, split_axis=2, concat_axis=0, tiled=True),
-        lax.all_to_all(local_term[None], GZ, split_axis=2, concat_axis=0, tiled=True),
+        jnp.concatenate(
+            lax.all_to_all(
+                jnp.stack(jnp.split(local_term[None], lax.axis_size(GZ), 2)),
+                split_axis=0,
+                axis_name=GZ,
+                concat_axis=0,
+            ),
+            0,
+        ),
     )
     got_decay = got_decay[:, :, 0]
     slice_width = got_term.shape[2]

time: 445 us -> 449 us (level)
    unnamed x82 -> x93, local copies, waits for them, and re-layouts: 3.92 us -> 8.61 us
    another operation x30 -> x31, local copies, waits for them, and re-layouts: 15.2 us -> 15.9 us
  transfers between devices with their start and end apart: 5 -> 5, of which waited for: 3 -> 3; matrix products, arithmetic and copies ran while one was open for 20% -> 21% of each run, Pallas kernels for 0% -> 0%
where the time goes in v1:
time: 449 us; the launch traced here: 445 us
  local copies, waits for them, and re-layouts  101 us (22%)
  other arithmetic  99 us (22%)
  blocking collectives  96.2 us (21%)
  matrix products  70.4 us (16%)
  waiting for transfers between devices  32.7 us (7%)
  starting transfers between devices  30.4 us (7%)
  between operations  14.6 us (3%)
    psum x5, blocking collectives, by_axis(): array = lax.psum(array, axis)  50.6 us
    all_gather x5, blocking collectives, carried_in(): pieces = jax.tree.map(lambda part: lax.all_gather(part, axis), so_far)  45.6 us
    dot_general x8, matrix products, block_forward(): inner = jnp.einsum('hts,shp->thp', mix, inputs, precision=highest)  40.7 us
    dynamic_update_slice x36, local copies, waits for them, and re-layouts, span_forward(): lax.map(one_block, (grouped, raw_g, read_g, decay_log.reshape(blocks, blo...  32.8 us
    dynamic_update_slice x24, other arithmetic, span_forward(): lax.map(one_block, (grouped, raw_g, read_g, decay_log.reshape(blocks, blo...  30.4 us
    all_to_all x1, waiting for transfers between devices, local(): lax.all_to_all(jnp.stack(jnp.split(local_term[None], lax.axis_size(GZ), 2...  29 us
    another operation x33, other arithmetic  27.7 us
    dot_general x8, matrix products, block_forward(): jnp.einsum('sh,shp,sn->hpn', tail, inputs, b_mat, precision=highest)  21.1 us
  transfers between devices with their start and end apart: 5, of which 3 were waited for; matrix products, arithmetic and copies ran while one was open for 21% of the time, Pallas kernels for 0%

profile of v1, /device:TPU:64, one launch (start us, length us, event | category | flops | bytes accessed | tf_op | source)
XLA Modules:
  0.0 445.0 jit_solution(16766089574438664800)
XLA Ops:
  10.4 11.8 %all-to-all-start.1 = ((f32[1,32,8]{1,0,2:T(1,128)}), f32[1,32,8]{1,0,2:T(1,128)S(1)}, u32[]{:S(2)}, u32[]{:S(2)}) async-start(f32[1,32,8]{1,0,2:T(1,128)} %broadcast_in_dim.210), calls=%async_computation.1 | async-start | bytes 8192 | tf_op jit(solution)/shard_map/all_to_all | solution.py:124
  22.4 1.5 copy.91
  30.5 1.8 all-to-all-done.1
  32.3 7.9 %all-to-all-start = ((f32[8,1,32,8,128]{4,3,2,1,0:T(8,128)}), f32[8,1,32,8,128]{4,3,2,1,0:T(8,128)S(1)}, u32[]{:S(2)}, u32[]{:S(2)}) async-start(f32[8,1,32,8,128]{4,3,2,1,0:T(8,128)} %fusion.85), calls=%async_computation | async-start | bytes 2097152 | tf_op jit(solution)/shard_map/all_to_all | solution.py:126
  41.5 29.0 %all-to-all-done = f32[8,1,32,8,128]{4,3,2,1,0:T(8,128)S(1)} async-done(((f32[8,1,32,8,128]{4,3,2,1,0:T(8,128)}), f32[8,1,32,8,128]{4,3,2,1,0:T(8,128)S(1)}, u32[]{:S(2)}, u32[]{:S(2)}) %all-to-all-start) | async-done | bytes 1048608 | tf_op jit(solution)/shard_map/all_to_all | solution.py:126
  71.6 4.3 all-to-all-start.3
  76.8 1.6 copy.87
  79.3 16.8 %all-gather = f32[8,1,32,1]{2,3,1,0:T(1,128)S(1)} all-gather(f32[1,1,32,1]{2,3,1,0:T(1,128)S(1)} %get-tuple-element.1740), channel_id=2, replica_groups=mesh['gx_0'=4,'gx_1'=2,'gy'=8,'gz_0'=4,'gz_1'=2] {'gy'}, dimensions={0}, use_global_device_ids=true | all-gather | bytes 1152 | tf_op jit(solution)/shard_map/all_gather | solution.py:24
  96.1 1.8 all-gather.1
  97.9 8.2 %all-gather.2 = f32[4,1,32]{2,1,0:T(1,128)S(1)} all-gather(f32[1,1,32]{2,1,0:T(1,128)S(1)} %get-tuple-element.1760), channel_id=1, replica_groups=mesh['gx_0'=4,'gx_1'=2,'gy'=8,'gz_0'=4,'gz_1'=2] {'gx_0'}, dimensions={0}, use_global_device_ids=true | all-gather | bytes 640 | tf_op jit(solution)/shard_map/all_gather | solution.py:24
  107.3 1.9 all-gather.5.cloned.1.call-done
  109.2 1.7 slice_add_fusion.6
  111.0 2.1 all_gather.28
  113.3 16.7 %all_gather.29 = f32[4,32,8,128]{3,2,1,0:T(8,128)S(1)} all-gather(f32[1,32,8,128]{3,2,1,0:T(8,128)S(1)} %slice_add_fusion.4), channel_id=1, replica_groups=mesh['gx_0'=4,'gx_1'=2,'gy'=8,'gz_0'=4,'gz_1'=2] {'gx_0'}, dimensions={0}, use_global_device_ids=true | all-gather | bytes 655360 | tf_op jit(solution)/shard_map/all_gather | solution.py:24
  130.1 2.2 add_dynamic-update-slice_fusion.6
  137.6 6.2 %all-to-all-start.2 = ((f32[8,32,8,128]{3,2,1,0:T(8,128)}), f32[8,32,8,128]{3,2,1,0:T(8,128)}, u32[]{:S(2)}, u32[]{:S(2)}) async-start(f32[8,32,8,128]{3,2,1,0:T(8,128)} %constant_dynamic-update-slice_fusion.3), calls=%async_computation.2 | async-start | bytes 2097152 | tf_op jit(solution)/shard_map/all_to_all | solution.py:155
  143.9 1.5 broadcast.740.clone.1
  149.1 57.5 %while.75 = (s32[]{:T(128)}, f32[4,256,8]{1,2,0:T(8,128)}, f32[4,8]{1,0:T(4,128)}, f32[4,1,8]{2,1,0:T(1,128)}, f32[4,256,8]{1,2,0:T(8,128)}, /*index=5*/f32[4,8,...) while((s32[]{:T(128)}, f32[4,256,8]{1,2,0:T(8,128)}, ...), condition=%wide.region_5.6_spmd.clone.clone, body=%wide.region_2.5_spmd.clone.clone.sunk | while | flops 3090474 | bytes 14180141 | solution.py:75
  150.7 4.2 multiply_dynamic-update-slice_fusion.4
  165.1 4.0 multiply_dynamic-update-slice_fusion.4
  179.5 4.1 multiply_dynamic-update-slice_fusion.4
  193.9 4.0 multiply_dynamic-update-slice_fusion.4
  212.1 1.8 convolution_bitcast_fusion.2
  213.9 2.3 copy.95
  216.3 1.5 broadcast.740
  220.1 157.2 %while.76 = (s32[]{:T(128)}, f32[256,256]{1,0:T(8,128)S(1)}, f32[256,128]{1,0:T(8,128)}, bf16[4,256,8,64]{1,3,2,0:T(8,128)(2,1)}, f32[4,256,8]{1,2,0:T(8,128)}, ...) while((s32[]{:T(128)}, f32[256,256]{1,0:T(8,128)S(1)}, ...), condition=%wide.region_19.20_spmd.clone.clone, body=%wide.region_6.19_spmd.clone.clone.sunk | while | flops 1215725568 | bytes 18326480 | solution.py:75
  220.7 2.5 fusion.160
  225.4 6.5 %fusion.158 = (f32[8,256]{1,0:T(8,128)}, f32[8,256]{1,0:T(8,128)}, f32[256,256]{1,0:T(8,128)S(1)}, f32[8,256]{1,0:T(8,128)}) fusion(f32[4,8,256,256]{3,2,1,0:T(8,128)} %get-tuple-element.2346, s32[]{:T(128)S(6)} %sub.146, f32[256,256]{1,0:T(8,128)S(1)} %bitcast.592, f32[8,256]{1,0:T(8,128)S(1)} %dynamic-slice_bitcast_fusion.6, ...), kind=kOutput, calls=%fused_computation.87.clone.1 | convolution fusion | flops 408348672 | bytes 7964160 | tf_op jit(solution)/shard_map/transpose(jvp())/while/body/eval_jaxpr/hts,shp->thp/dot_general | solution.py:50
  231.9 1.7 fusion.165
  235.6 1.4 fusion.167
  237.1 3.1 reduce-window.62
  243.4 1.4 fusion.168
  250.0 3.7 fusion.162
  256.6 2.8 fusion.159
  260.0 2.5 fusion.160
  264.7 6.5 %fusion.158 = (f32[8,256]{1,0:T(8,128)}, f32[8,256]{1,0:T(8,128)}, f32[256,256]{1,0:T(8,128)S(1)}, f32[8,256]{1,0:T(8,128)}) fusion(f32[4,8,256,256]{3,2,1,0:T(8,128)} %get-tuple-element.2346, s32[]{:T(128)S(6)} %sub.146, f32[256,256]{1,0:T(8,128)S(1)} %bitcast.592, f32[8,256]{1,0:T(8,128)S(1)} %dynamic-slice_bitcast_fusion.6, ...), kind=kOutput, calls=%fused_computation.87.clone.1 | convolution fusion | flops 408348672 | bytes 7964160 | tf_op jit(solution)/shard_map/transpose(jvp())/while/body/eval_jaxpr/hts,shp->thp/dot_general | solution.py:50
  271.1 1.7 fusion.165
  276.3 3.1 reduce-window.62
  282.7 1.4 fusion.168
  289.3 3.7 fusion.162
  295.9 2.8 fusion.159
  299.3 2.5 fusion.160
  304.0 6.5 %fusion.158 = (f32[8,256]{1,0:T(8,128)}, f32[8,256]{1,0:T(8,128)}, f32[256,256]{1,0:T(8,128)S(1)}, f32[8,256]{1,0:T(8,128)}) fusion(f32[4,8,256,256]{3,2,1,0:T(8,128)} %get-tuple-element.2346, s32[]{:T(128)S(6)} %sub.146, f32[256,256]{1,0:T(8,128)S(1)} %bitcast.592, f32[8,256]{1,0:T(8,128)S(1)} %dynamic-slice_bitcast_fusion.6, ...), kind=kOutput, calls=%fused_computation.87.clone.1 | convolution fusion | flops 408348672 | bytes 7964160 | tf_op jit(solution)/shard_map/transpose(jvp())/while/body/eval_jaxpr/hts,shp->thp/dot_general | solution.py:50
  310.5 1.7 fusion.165
  314.2 1.4 fusion.167
  315.7 3.1 reduce-window.62
  322.1 1.4 fusion.168
  328.6 3.7 fusion.162
  335.3 2.8 fusion.159
  338.7 2.5 fusion.160
  343.4 6.5 %fusion.158 = (f32[8,256]{1,0:T(8,128)}, f32[8,256]{1,0:T(8,128)}, f32[256,256]{1,0:T(8,128)S(1)}, f32[8,256]{1,0:T(8,128)}) fusion(f32[4,8,256,256]{3,2,1,0:T(8,128)} %get-tuple-element.2346, s32[]{:T(128)S(6)} %sub.146, f32[256,256]{1,0:T(8,128)S(1)} %bitcast.592, f32[8,256]{1,0:T(8,128)S(1)} %dynamic-slice_bitcast_fusion.6, ...), kind=kOutput, calls=%fused_computation.87.clone.1 | convolution fusion | flops 408348672 | bytes 7964160 | tf_op jit(solution)/shard_map/transpose(jvp())/while/body/eval_jaxpr/hts,shp->thp/dot_general | solution.py:50
  349.8 1.7 fusion.165
  355.0 3.1 reduce-window.62
  361.4 1.4 fusion.168
  367.9 3.7 fusion.162
  374.6 2.8 fusion.159
  380.9 1.9 convolution_add_fusion.1
  382.9 2.3 copy.98
  385.1 11.9 %all-reduce.4 = (f32[32]{0:T(128)S(1)}, f32[32]{0:T(128)S(1)}, f32[32]{0:T(128)S(1)}) all-reduce(f32[32]{0:T(128)S(1)} %reshape.896, f32[32]{0:T(128)S(1)} %reshape.897, f32[32]{0:T(128)S(1)} %reshape.898), channel_id=1, replica_groups=mesh['gx_0'=4,'gx_1'=2,'gy'=8,'gz_0'=4,'gz_1'=2] {'gx_0'}, use_global_device_ids=true, to_apply=%region_20.21 | all-reduce | flops 96 | bytes 768 | tf_op jit(solution)/shard_map/psum | solution.py:36
  397.0 2.5 all-reduce.6
  399.5 15.9 %all-reduce.2 = (f32[32]{0:T(128)S(1)}, f32[32]{0:T(128)S(1)}, f32[32]{0:T(128)S(1)}) all-reduce(f32[32]{0:T(128)S(1)} %get-tuple-element.1697, f32[32]{0:T(128)S(1)} %get-tuple-element.1698, f32[32]{0:T(128)S(1)} %get-tuple-element.1699), channel_id=1, replica_groups=mesh['gx_0'=4,'gx_1'=2,'gy'=8,'gz_0'=4,'gz_1'=2] {'gy'}, use_global_device_ids=true, to_apply=%region_22.23 | all-reduce | flops 96 | bytes 768 | tf_op jit(solution)/shard_map/psum | solution.py:36
  415.4 10.9 %all-reduce.3 = (f32[32]{0:T(128)S(1)}, f32[32]{0:T(128)S(1)}, f32[32]{0:T(128)S(1)}) all-reduce(f32[32]{0:T(128)S(1)} %get-tuple-element.1685, f32[32]{0:T(128)S(1)} %get-tuple-element.1686, f32[32]{0:T(128)S(1)} %get-tuple-element.1687), channel_id=1, replica_groups=mesh['gx_0'=4,'gx_1'=2,'gy'=8,'gz_0'=4,'gz_1'=2] {'gz_0'}, use_global_device_ids=true, to_apply=%region_23.24 | all-reduce | flops 96 | bytes 768 | tf_op jit(solution)/shard_map/psum | solution.py:36
  426.3 9.3 %all-reduce.5 = (f32[32]{0:T(128)}, f32[32]{0:T(128)}, f32[32]{0:T(128)}) all-reduce(f32[32]{0:T(128)S(1)} %get-tuple-element.1688, f32[32]{0:T(128)S(1)} %get-tuple-element.1689, f32[32]{0:T(128)S(1)} %get-tuple-element.1690), channel_id=1, replica_groups=mesh['gx_0'=4,'gx_1'=2,'gy'=8,'gz_0'=4,'gz_1'=2] {'gz_1'}, use_global_device_ids=true, to_apply=%region_24.25 | all-reduce | flops 96 | bytes 768 | tf_op jit(solution)/shard_map/psum | solution.py:36
  435.7 2.5 convolution_add_fusion
  (350 shorter events, 143.8 us)
Async XLA Ops:
  7.2 16.8 %copy-start = (bf16[256,128]{1,0:T(8,128)(2,1)S(1)}, bf16[256,128]{1,0:T(8,128)(2,1)}, u32[]{:S(2)}) copy-start(bf16[256,128]{1,0:T(8,128)(2,1)} %param.16) | copy-start | bytes 196612
  10.4 21.9 %all-to-all-start.1 = ((f32[1,32,8]{1,0,2:T(1,128)}), f32[1,32,8]{1,0,2:T(1,128)S(1)}, u32[]{:S(2)}, u32[]{:S(2)}) async-start(f32[1,32,8]{1,0,2:T(1,128)} %broadcast_in_dim.210), calls=%async_computation.1 | async-start | bytes 8192 | tf_op jit(solution)/shard_map/all_to_all | solution.py:124
  23.8 1.2 copy-start.1
  30.5 45.6 %copy-start.33 = (f32[32]{0:T(128)S(1)}, f32[32]{0:T(128)}, u32[]{:S(2)}) copy-start(f32[32]{0:T(128)} %param.18) | copy-start | bytes 388
  30.5 46.2 %copy-start.43 = (f32[32]{0:T(128)S(1)}, f32[32]{0:T(128)}, u32[]{:S(2)}) copy-start(f32[32]{0:T(128)} %param.17) | copy-start | bytes 388
  30.5 46.3 %copy-start.8 = (bf16[256,2048]{1,0:T(8,128)(2,1)S(1)}, bf16[256,2048]{1,0:T(8,128)(2,1)}, u32[]{:S(2)}) copy-start(bf16[256,2048]{1,0:T(8,128)(2,1)} %param.13) | copy-start | bytes 3145732
  32.3 38.2 %all-to-all-start = ((f32[8,1,32,8,128]{4,3,2,1,0:T(8,128)}), f32[8,1,32,8,128]{4,3,2,1,0:T(8,128)S(1)}, u32[]{:S(2)}, u32[]{:S(2)}) async-start(f32[8,1,32,8,128]{4,3,2,1,0:T(8,128)} %fusion.85), calls=%async_computation | async-start | bytes 2097152 | tf_op jit(solution)/shard_map/all_to_all | solution.py:126
  40.2 68.9 %all-gather.5.cloned.1.call-start = ((), (), s32[]{:S(2)}) async-start(), calls=%async_computation.4 | async-start | bytes 1179648 | tf_op jit(solution)/shard_map/all_gather | solution.py:24
  40.9 37.5 %copy-start.19 = (f32[32]{0:T(128)}, f32[32]{0:T(128)S(1)}, u32[]{:S(2)}) copy-start(f32[32]{0:T(128)S(1)} %get-tuple-element.1755) | copy-start | bytes 388
  41.5 36.9 %copy-start.21 = (f32[32]{0:T(128)}, f32[32]{0:T(128)S(1)}, u32[]{:S(2)}) copy-start(f32[32]{0:T(128)S(1)} %get-tuple-element.1746) | copy-start | bytes 388
  41.5 36.9 %copy-start.24 = (f32[32]{0:T(128)}, f32[32]{0:T(128)S(1)}, u32[]{:S(2)}) copy-start(f32[32]{0:T(128)S(1)} %get-tuple-element.1742) | copy-start | bytes 388
  41.5 36.9 %copy-start.26 = (f32[32]{0:T(128)}, f32[32]{0:T(128)S(1)}, u32[]{:S(2)}) copy-start(f32[32]{0:T(128)S(1)} %get-tuple-element.1744) | copy-start | bytes 388
  71.6 6.8 %copy-start.44 = (f32[32]{0:T(128)S(1)}, f32[32]{0:T(128)}, u32[]{:S(2)}) copy-start(f32[32]{0:T(128)} %param.19) | copy-start | bytes 388
  71.6 7.5 %copy-start.10 = (bf16[256,128]{1,0:T(8,128)(2,1)S(1)}, bf16[256,128]{1,0:T(8,128)(2,1)}, u32[]{:S(2)}) copy-start(bf16[256,128]{1,0:T(8,128)(2,1)} %param.15) | copy-start | bytes 196612
  71.6 66.0 %all-to-all-start.3 = ((bf16[8,32,8,128]{3,2,1,0:T(8,128)(2,1)}), bf16[8,32,8,128]{3,2,1,0:T(8,128)(2,1)}, u32[]{:S(2)}, u32[]{:S(2)}) async-start(bf16[8,32,8,128]{3,2,1,0:T(8,128)(2,1)} %param.20), calls=%async_computation.3 | async-start | bytes 1048576 | tf_op jit(solution)/shard_map/all_to_all | solution.py:106
  96.1 14.8 %copy-start.15 = (f32[32]{0:T(128)}, f32[32]{0:T(128)S(1)}, u32[]{:S(2)}) copy-start(f32[32]{0:T(128)S(1)} %get-tuple-element.1750) | copy-start | bytes 388
  96.1 14.8 %copy-start.16 = (f32[32]{0:T(128)}, f32[32]{0:T(128)S(1)}, u32[]{:S(2)}) copy-start(f32[32]{0:T(128)S(1)} %get-tuple-element.1751) | copy-start | bytes 388
  96.1 14.8 %copy-start.17 = (f32[32]{0:T(128)}, f32[32]{0:T(128)S(1)}, u32[]{:S(2)}) copy-start(f32[32]{0:T(128)S(1)} %get-tuple-element.1753) | copy-start | bytes 388
  96.1 14.8 %copy-start.18 = (f32[32]{0:T(128)}, f32[32]{0:T(128)S(1)}, u32[]{:S(2)}) copy-start(f32[32]{0:T(128)S(1)} %get-tuple-element.1754) | copy-start | bytes 388
  97.9 15.2 %copy-start.23 = (f32[32]{0:T(128)}, f32[32]{0:T(128)S(1)}, u32[]{:S(2)}) copy-start(f32[32]{0:T(128)S(1)} %get-tuple-element.1761) | copy-start | bytes 388
  106.1 4.8 %copy-start.28 = (f32[32]{0:T(128)}, f32[32]{0:T(128)S(1)}, u32[]{:S(2)}) copy-start(f32[32]{0:T(128)S(1)} %bitcast_multiply_fusion.15) | copy-start | bytes 388
  106.1 7.0 %copy-start.29 = (f32[32]{0:T(128)}, f32[32]{0:T(128)S(1)}, u32[]{:S(2)}) copy-start(f32[32]{0:T(128)S(1)} %bitcast_multiply_fusion.17) | copy-start | bytes 388
  109.1 20.9 %copy-start.5 = (f32[8,32,8,128]{3,2,1,0:T(8,128)S(1)}, f32[8,32,8,128]{3,2,1,0:T(8,128)}, u32[]{:S(2)}) copy-start(f32[8,32,8,128]{3,2,1,0:T(8,128)} %all-gather.5.cloned.1.call-done) | copy-start | bytes 3145732
  109.1 20.9 %copy-start.22 = (f32[32]{0:T(128)S(1)}, f32[32]{0:T(128)}, u32[]{:S(2)}) copy-start(f32[32]{0:T(128)} %copy-done.21) | copy-start | bytes 388
  109.1 20.9 %copy-start.35 = (f32[32]{0:T(128)S(1)}, f32[32]{0:T(128)}, u32[]{:S(2)}) copy-start(f32[32]{0:T(128)} %get-tuple-element.1716) | copy-start | bytes 388
  109.1 20.9 %copy-start.36 = (f32[32]{0:T(128)S(1)}, f32[32]{0:T(128)}, u32[]{:S(2)}) copy-start(f32[32]{0:T(128)} %get-tuple-element.1717) | copy-start | bytes 388
  109.1 20.9 %copy-start.37 = (f32[32]{0:T(128)S(1)}, f32[32]{0:T(128)}, u32[]{:S(2)}) copy-start(f32[32]{0:T(128)} %get-tuple-element.1756) | copy-start | bytes 388
  109.2 20.9 %copy-start.38 = (f32[32]{0:T(128)S(1)}, f32[32]{0:T(128)}, u32[]{:S(2)}) copy-start(f32[32]{0:T(128)} %get-tuple-element.1757) | copy-start | bytes 388
  109.2 20.9 %copy-start.39 = (f32[32]{0:T(128)S(1)}, f32[32]{0:T(128)}, u32[]{:S(2)}) copy-start(f32[32]{0:T(128)} %get-tuple-element.1758) | copy-start | bytes 388
  109.2 20.9 %copy-start.40 = (f32[32]{0:T(128)S(1)}, f32[32]{0:T(128)}, u32[]{:S(2)}) copy-start(f32[32]{0:T(128)} %get-tuple-element.1759) | copy-start | bytes 388
  110.9 21.4 %copy-start.32 = (f32[32]{0:T(128)S(1)}, f32[32]{0:T(128)}, u32[]{:S(2)}) copy-start(f32[32]{0:T(128)} %get-tuple-element.1711) | copy-start | bytes 388
  110.9 22.1 %copy-start.7 = (f32[1,32,8,128]{3,2,1,0:T(8,128)S(1)}, f32[1,32,8,128]{3,2,1,0:T(8,128)}, u32[]{:S(2)}) copy-start(f32[1,32,8,128]{3,2,1,0:T(8,128)} %get-tuple-element.1722) | copy-start | bytes 393220
  111.0 22.1 %copy-start.27 = (f32[32]{0:T(128)S(1)}, f32[32]{0:T(128)}, u32[]{:S(2)}) copy-start(f32[32]{0:T(128)} %copy-done.26) | copy-start | bytes 388
  111.0 22.1 %copy-start.42 = (f32[32]{0:T(128)S(1)}, f32[32]{0:T(128)}, u32[]{:S(2)}) copy-start(f32[32]{0:T(128)} %get-tuple-element.1712) | copy-start | bytes 388
  113.1 20.8 %copy-start.31 = (f32[32]{0:T(128)S(1)}, f32[32]{0:T(128)}, u32[]{:S(2)}) copy-start(f32[32]{0:T(128)} %get-tuple-element.1713) | copy-start | bytes 388
  113.3 21.4 %copy-start.6 = (f32[1,32,8,128]{3,2,1,0:T(8,128)S(1)}, f32[1,32,8,128]{3,2,1,0:T(8,128)}, u32[]{:S(2)}) copy-start(f32[1,32,8,128]{3,2,1,0:T(8,128)} %get-tuple-element.1723) | copy-start | bytes 393220
  113.3 21.4 %copy-start.25 = (f32[32]{0:T(128)S(1)}, f32[32]{0:T(128)}, u32[]{:S(2)}) copy-start(f32[32]{0:T(128)} %copy-done.24) | copy-start | bytes 388
  113.3 21.4 %copy-start.41 = (f32[32]{0:T(128)S(1)}, f32[32]{0:T(128)}, u32[]{:S(2)}) copy-start(f32[32]{0:T(128)} %get-tuple-element.1714) | copy-start | bytes 388
  130.1 5.4 %copy-start.30 = (f32[32]{0:T(128)S(1)}, f32[32]{0:T(128)}, u32[]{:S(2)}) copy-start(f32[32]{0:T(128)} %get-tuple-element.1715) | copy-start | bytes 388
  130.1 6.1 %copy-start.20 = (f32[32]{0:T(128)S(1)}, f32[32]{0:T(128)}, u32[]{:S(2)}) copy-start(f32[32]{0:T(128)} %copy-done.19) | copy-start | bytes 388
  130.1 6.1 %copy-start.34 = (f32[32]{0:T(128)S(1)}, f32[32]{0:T(128)}, u32[]{:S(2)}) copy-start(f32[32]{0:T(128)} %get-tuple-element.1738) | copy-start | bytes 388
  137.6 11.4 %copy-start.9 = (f32[256,32]{0,1:T(8,128)S(1)}, f32[256,32]{0,1:T(8,128)}, u32[]{:S(2)}) copy-start(f32[256,32]{0,1:T(8,128)} %param.14) | copy-start | bytes 98308
  137.6 76.3 %all-to-all-start.2 = ((f32[8,32,8,128]{3,2,1,0:T(8,128)}), f32[8,32,8,128]{3,2,1,0:T(8,128)}, u32[]{:S(2)}, u32[]{:S(2)}) async-start(f32[8,32,8,128]{3,2,1,0:T(8,128)} %constant_dynamic-update-slice_fusion.3), calls=%async_computation.2 | async-start | bytes 2097152 | tf_op jit(solution)/shard_map/all_to_all | solution.py:155
  206.5 1.4 copy-start.11
  211.0 3.0 copy-start.3
  220.1 0.6 copy-start.12
  250.0 3.8 copy-start.14
  253.7 5.7 %copy-start.13 = (f32[4,8]{0,1:T(8,128)S(1)}, f32[4,8]{0,1:T(8,128)}, u32[]{:S(2)}) copy-start(f32[4,8]{0,1:T(8,128)} %copy-done.12) | copy-start | bytes 388 | tf_op jit(solution)/shard_map/transpose(jvp())/while
  259.4 0.6 copy-start.12
  289.3 3.8 copy-start.14
  293.0 5.7 %copy-start.13 = (f32[4,8]{0,1:T(8,128)S(1)}, f32[4,8]{0,1:T(8,128)}, u32[]{:S(2)}) copy-start(f32[4,8]{0,1:T(8,128)} %copy-done.12) | copy-start | bytes 388 | tf_op jit(solution)/shard_map/transpose(jvp())/while
  298.7 0.6 copy-start.12
  328.6 3.8 copy-start.14
  332.4 5.7 %copy-start.13 = (f32[4,8]{0,1:T(8,128)S(1)}, f32[4,8]{0,1:T(8,128)}, u32[]{:S(2)}) copy-start(f32[4,8]{0,1:T(8,128)} %copy-done.12) | copy-start | bytes 388 | tf_op jit(solution)/shard_map/transpose(jvp())/while
  338.1 0.6 copy-start.12
  367.9 3.8 copy-start.14
  371.6 5.7 %copy-start.13 = (f32[4,8]{0,1:T(8,128)S(1)}, f32[4,8]{0,1:T(8,128)}, u32[]{:S(2)}) copy-start(f32[4,8]{0,1:T(8,128)} %copy-done.12) | copy-start | bytes 388 | tf_op jit(solution)/shard_map/transpose(jvp())/while
  377.4 58.3 %copy-start.2 = (f32[4,256,8,64]{1,3,2,0:T(8,128)S(1)}, f32[4,256,8,64]{1,3,2,0:T(8,128)}, u32[]{:S(2)}) copy-start(f32[4,256,8,64]{1,3,2,0:T(8,128)} %get-tuple-element.1033) | copy-start | bytes 6291460
  377.4 58.3 %copy-start.4 = (bf16[8,32,8,128]{3,2,0,1:T(8,128)(2,1)S(1)}, bf16[8,32,8,128]{3,2,0,1:T(8,128)(2,1)}, u32[]{:S(2)}) copy-start(bf16[8,32,8,128]{3,2,0,1:T(8,128)(2,1)} %copy-done.3) | copy-start | bytes 1572868
Sparse Core Ops, SparseCore 0:
  71.7 37.4 all-gather.4
